TPU v7x, 32 devices: a whole 2x2x4 slice. The times are simulated.
32 devices in a mesh: rows: 4 (over x, core), seq: 8 (over z, y).
Axes of the slice: x: 2, y: 2, z: 4, core: 2. Of those that a mesh axis runs over, the one named last changes fastest.
Arguments:
- layer_in: bfloat16 [32, 1024, 768], P('rows', 'seq'), may hold values from -6 to 6
- cotangent: bfloat16 [32, 1024, 768], P('rows', 'seq'), may hold values from -6 to 6
- seg_lengths: int32 [32, 4], P('rows'), may hold values from 1 to 384, as said below
- query_weight: bfloat16 [768, 768], P(('rows', 'seq')), may hold values from -0.21875 to 0.21875
- query_bias: bfloat16 [768], P(('rows', 'seq')), may hold values from -3 to 3
- key_weight: bfloat16 [768, 768], P(('rows', 'seq')), may hold values from -0.21875 to 0.21875
- value_weight: bfloat16 [768, 768], P(('rows', 'seq')), may hold values from -0.21875 to 0.21875
- value_bias: bfloat16 [768], P(('rows', 'seq')), may hold values from -3 to 3
- out_weight: bfloat16 [768, 768], P(('rows', 'seq')), may hold values from -0.875 to 0.875
- out_bias: bfloat16 [768], P(('rows', 'seq')), may hold values from -2 to 2
- attn_gain: bfloat16 [768], P(('rows', 'seq')), may hold values from 0.5 to 1.5
- attn_shift: bfloat16 [768], P(('rows', 'seq')), may hold values from -2 to 2
- inner_weight: bfloat16 [768, 3072], P(('rows', 'seq')), may hold values from -0.21875 to 0.21875
- inner_bias: bfloat16 [3072], P(('rows', 'seq')), may hold values from -3 to 3
- outer_weight: bfloat16 [3072, 768], P(('rows', 'seq')), may hold values from -0.21875 to 0.21875
- outer_bias: bfloat16 [768], P(('rows', 'seq')), may hold values from -2 to 2
- final_gain: bfloat16 [768], P(('rows', 'seq')), may hold values from 0.5 to 1.5
- final_shift: bfloat16 [768], P(('rows', 'seq')), may hold values from -2 to 2
Outputs:
- layer_out: bfloat16 [32, 1024, 768], P('rows', 'seq')
- grad_in: float32 [32, 1024, 768], P('rows', 'seq')
- grad_query_weight: float32 [768, 768], P(('rows', 'seq'))
- grad_query_bias: float32 [768], P(('rows', 'seq'))
- grad_key_weight: float32 [768, 768], P(('rows', 'seq'))
- grad_value_weight: float32 [768, 768], P(('rows', 'seq'))
- grad_value_bias: float32 [768], P(('rows', 'seq'))
- grad_out_weight: float32 [768, 768], P(('rows', 'seq'))
- grad_out_bias: float32 [768], P(('rows', 'seq'))
- grad_attn_gain: float32 [768], P(('rows', 'seq'))
- grad_attn_shift: float32 [768], P(('rows', 'seq'))
- grad_inner_weight: float32 [768, 3072], P(('rows', 'seq'))
- grad_inner_bias: float32 [3072], P(('rows', 'seq'))
- grad_outer_weight: float32 [3072, 768], P(('rows', 'seq'))
- grad_outer_bias: float32 [768], P(('rows', 'seq'))
- grad_final_gain: float32 [768], P(('rows', 'seq'))
- grad_final_shift: float32 [768], P(('rows', 'seq'))
Inputs may be any that keep to these rules, and one draw needn't show every extreme that they name: `seg_lengths`: the lengths of each row sum to 960, and the positions past their sum are padding; the last segment of each row has exactly 384 tokens.
All inputs are finite; a program needn't handle non-finite values.
Results may differ from a plain program's by a relative error of at most 0.015.
Values may be sent and summed in bfloat16 or wider, within the bound.
A program may use at most 256 MiB of HBM per device.

v0:
```python
from functools import partial
import jax
import jax.numpy as jnp
from jax import lax
from jax.sharding import PartitionSpec as P

HEADS = 12
HEAD_DIM = 64
REACH = 3
epsilon = 1e-12
masked_score = -1e30


def passed_along(block, axis, distance):
    devices = range(lax.axis_size(axis))
    route = [(i - distance, i) for i in devices if i - distance in devices]
    return lax.ppermute(block, axis, route)


def segment_ids(lengths, positions, row_len):
    seg_ends = jnp.cumsum(lengths, axis=1)
    seg_count = jnp.sum(
        (positions[None, None, :] >= seg_ends[:, :, None]).astype(jnp.int32), axis=1
    )
    real_token = positions[None, :] < seg_ends[:, -1:]
    inside = (positions >= 0) & (positions < row_len)
    seg_id = jnp.where(real_token, seg_count, row_len + positions[None, :])
    return jnp.where(inside[None, :], seg_id, -1)


def norm_parts(values):
    row_mean = jnp.mean(values, axis=-1, keepdims=True)
    centred = values - row_mean
    inv_std = lax.rsqrt(jnp.mean(centred * centred, axis=-1, keepdims=True) + epsilon)
    return (centred * inv_std, inv_std)


def norm_back(upstream, normed, inv_std, gain_vec):
    scaled = upstream * gain_vec
    return inv_std * (
        scaled
        - jnp.mean(scaled, axis=-1, keepdims=True)
        - normed * jnp.mean(scaled * normed, axis=-1, keepdims=True)
    )


def split_window(window, features):
    key_rows = window[:, :features].reshape(window.shape[0], HEADS, HEAD_DIM)
    value_rows = window[:, features:].reshape(window.shape[0], HEADS, HEAD_DIM)
    return (key_rows, value_rows)


def row_scores(query_rows, key_rows, same_segment, score_scale):
    scores = (
        jnp.einsum("qhd,khd->hqk", query_rows, key_rows, preferred_element_type=jnp.float32)
        * score_scale
    )
    return jnp.where(same_segment[None], scores, masked_score)


def attend_row(pieces, score_scale):
    query_rows, window, same_segment = pieces
    key_rows, value_rows = split_window(window, query_rows.shape[1] * query_rows.shape[2])
    scores = row_scores(query_rows, key_rows, same_segment, score_scale)
    row_max = jnp.max(scores, axis=-1, keepdims=True)
    weights = jnp.exp(scores - row_max)
    row_total = jnp.sum(weights, axis=-1, keepdims=True)
    weights_b = (weights / row_total).astype(jnp.bfloat16)
    context = jnp.einsum("hqk,khd->qhd", weights_b, value_rows, preferred_element_type=jnp.float32)
    return (context.astype(jnp.bfloat16), (row_max + jnp.log(row_total))[..., 0])


def attend_back(pieces, score_scale):
    query_rows, window, same_segment, logsum, grad_context = pieces
    features = query_rows.shape[1] * query_rows.shape[2]
    key_rows, value_rows = split_window(window, features)
    scores = row_scores(query_rows, key_rows, same_segment, score_scale)
    probs = jnp.exp(scores - logsum[..., None])
    grad_probs = jnp.einsum(
        "qhd,khd->hqk", grad_context, value_rows, preferred_element_type=jnp.float32
    )
    grad_scores = (
        probs * (grad_probs - jnp.sum(grad_probs * probs, axis=-1, keepdims=True))
    ).astype(jnp.bfloat16)
    grad_query = (
        jnp.einsum("hqk,khd->qhd", grad_scores, key_rows, preferred_element_type=jnp.float32)
        * score_scale
    )
    grad_key = (
        jnp.einsum("hqk,qhd->khd", grad_scores, query_rows, preferred_element_type=jnp.float32)
        * score_scale
    )
    grad_value = jnp.einsum(
        "hqk,qhd->khd", probs.astype(jnp.bfloat16), grad_context, preferred_element_type=jnp.float32
    )
    width_keys = window.shape[0]
    return (
        grad_query,
        jnp.concatenate(
            [grad_key.reshape(width_keys, features), grad_value.reshape(width_keys, features)],
            axis=1,
        ),
    )


def near_distances():
    return list(range(REACH, 0, -1)) + list(range(-1, -REACH - 1, -1))


def near_window(kv_local):
    lower_side = []
    upper_side = []
    for distance in near_distances():
        arrived = passed_along(kv_local, "seq", distance)
        if distance > 0:
            lower_side.append(arrived)
        else:
            upper_side.append(arrived)
    return jnp.concatenate(lower_side + [kv_local] + upper_side, axis=1)


def near_back(grad_window, block_len):
    own_grad = grad_window[:, REACH * block_len : (REACH + 1) * block_len]
    for position in range(2 * REACH + 1):
        offset = position - REACH
        if offset != 0:
            grad_piece = grad_window[:, position * block_len : (position + 1) * block_len]
            own_grad = own_grad + passed_along(
                grad_piece.astype(jnp.bfloat16), "seq", offset
            ).astype(grad_piece.dtype)
    return own_grad


def body(
    layer_in,
    cotangent,
    seg_lengths,
    query_weight,
    query_bias,
    key_weight,
    value_weight,
    value_bias,
    out_weight,
    out_bias,
    attn_gain,
    attn_shift,
    inner_weight,
    inner_bias,
    outer_weight,
    outer_bias,
    final_gain,
    final_shift,
):
    shards = (
        query_weight,
        query_bias,
        key_weight,
        value_weight,
        value_bias,
        out_weight,
        out_bias,
        attn_gain,
        attn_shift,
        inner_weight,
        inner_bias,
        outer_weight,
        outer_bias,
        final_gain,
        final_shift,
    )
    gathered = (
        lax.all_gather(shards[0], ("rows", "seq"), axis=0, tiled=True),
        lax.all_gather(shards[1], ("rows", "seq"), axis=0, tiled=True),
        lax.all_gather(shards[2], ("rows", "seq"), axis=0, tiled=True),
        lax.all_gather(shards[3], ("rows", "seq"), axis=0, tiled=True),
        lax.all_gather(shards[4], ("rows", "seq"), axis=0, tiled=True),
        lax.all_gather(shards[5], ("rows", "seq"), axis=0, tiled=True),
        lax.all_gather(shards[6], ("rows", "seq"), axis=0, tiled=True),
        lax.all_gather(shards[7], ("rows", "seq"), axis=0, tiled=True),
        lax.all_gather(shards[8], ("rows", "seq"), axis=0, tiled=True),
        lax.all_gather(shards[9], ("rows", "seq"), axis=0, tiled=True),
        lax.all_gather(shards[10], ("rows", "seq"), axis=0, tiled=True),
        lax.all_gather(shards[11], ("rows", "seq"), axis=0, tiled=True),
        lax.all_gather(shards[12], ("rows", "seq"), axis=0, tiled=True),
        lax.all_gather(shards[13], ("rows", "seq"), axis=0, tiled=True),
        lax.all_gather(shards[14], ("rows", "seq"), axis=0, tiled=True),
    )
    (
        query_mat,
        query_vec,
        key_mat,
        value_mat,
        value_vec,
        out_mat,
        out_vec,
        attn_gain_f,
        attn_shift_f,
        inner_mat,
        inner_vec,
        outer_mat,
        outer_vec,
        final_gain_f,
        final_shift_f,
    ) = gathered
    row_count, block_len, features = layer_in.shape
    tokens = row_count * block_len
    score_scale = HEAD_DIM ** (-0.5)
    inputs = layer_in.reshape(tokens, features)
    query_flat = jnp.dot(inputs, query_mat, preferred_element_type=jnp.float32) + query_vec.astype(
        jnp.float32
    )
    query_b = query_flat.astype(jnp.bfloat16).reshape(row_count, block_len, HEADS, HEAD_DIM)
    kv_mat = jnp.concatenate([key_mat, value_mat], axis=1)
    kv_bias = jnp.concatenate([jnp.zeros_like(value_vec), value_vec]).astype(jnp.float32)
    kv_local = (
        (jnp.dot(inputs, kv_mat, preferred_element_type=jnp.float32) + kv_bias)
        .astype(jnp.bfloat16)
        .reshape(row_count, block_len, 2 * features)
    )
    seq_index = lax.axis_index("seq")
    row_len = block_len * lax.axis_size("seq")
    local_pos = seq_index * block_len + jnp.arange(block_len, dtype=jnp.int32)
    window_pos = (seq_index - REACH) * block_len + jnp.arange(
        (2 * REACH + 1) * block_len, dtype=jnp.int32
    )
    query_ids = segment_ids(seg_lengths, local_pos, row_len)
    key_ids = segment_ids(seg_lengths, window_pos, row_len)
    same_segment = query_ids[:, :, None] == key_ids[:, None, :]
    window = near_window(kv_local)
    context, logsum = lax.map(
        partial(attend_row, score_scale=score_scale), (query_b, window, same_segment)
    )
    context_flat = context.reshape(tokens, features)
    attended = jnp.dot(context_flat, out_mat, preferred_element_type=jnp.float32) + out_vec.astype(
        jnp.float32
    )
    first_sum = inputs.astype(jnp.float32) + attended
    normed_one, inv_std_one = norm_parts(first_sum)
    hidden = normed_one * attn_gain_f.astype(jnp.float32) + attn_shift_f.astype(jnp.float32)
    hidden_b = hidden.astype(jnp.bfloat16)
    inner_pre = jnp.dot(hidden_b, inner_mat, preferred_element_type=jnp.float32) + inner_vec.astype(
        jnp.float32
    )
    active, gelu_back = jax.vjp(partial(jax.nn.gelu, approximate=False), inner_pre)
    active_b = active.astype(jnp.bfloat16)
    outer_out = jnp.dot(active_b, outer_mat, preferred_element_type=jnp.float32) + outer_vec.astype(
        jnp.float32
    )
    normed_two, inv_std_two = norm_parts(hidden + outer_out)
    layer_out = (
        normed_two * final_gain_f.astype(jnp.float32) + final_shift_f.astype(jnp.float32)
    ).astype(jnp.bfloat16)
    real_token = (local_pos[None, :] < jnp.sum(seg_lengths, axis=1)[:, None]).astype(jnp.float32)
    upstream = (cotangent.astype(jnp.float32) * real_token[:, :, None]).reshape(tokens, features)
    grad_final_gain = jnp.sum(upstream * normed_two, axis=0)
    grad_final_shift = jnp.sum(upstream, axis=0)
    grad_second = norm_back(upstream, normed_two, inv_std_two, final_gain_f.astype(jnp.float32))
    grad_outer = grad_second.astype(jnp.bfloat16)
    grad_outer_bias = jnp.sum(grad_outer.astype(jnp.float32), axis=0)
    grad_outer_weight = jnp.einsum(
        "tf,td->fd", active_b, grad_outer, preferred_element_type=jnp.float32
    )
    grad_active = jnp.einsum("td,fd->tf", grad_outer, outer_mat, preferred_element_type=jnp.float32)
    grad_inner = gelu_back(grad_active)[0].astype(jnp.bfloat16)
    grad_inner_bias = jnp.sum(grad_inner.astype(jnp.float32), axis=0)
    grad_inner_weight = jnp.einsum(
        "td,tf->df", hidden_b, grad_inner, preferred_element_type=jnp.float32
    )
    grad_hidden = grad_second + jnp.einsum(
        "tf,df->td", grad_inner, inner_mat, preferred_element_type=jnp.float32
    )
    grad_attn_gain = jnp.sum(grad_hidden * normed_one, axis=0)
    grad_attn_shift = jnp.sum(grad_hidden, axis=0)
    grad_first = norm_back(grad_hidden, normed_one, inv_std_one, attn_gain_f.astype(jnp.float32))
    grad_attended = grad_first.astype(jnp.bfloat16)
    grad_out_bias = jnp.sum(grad_attended.astype(jnp.float32), axis=0)
    grad_out_weight = jnp.einsum(
        "td,te->de", context_flat, grad_attended, preferred_element_type=jnp.float32
    )
    grad_context = jnp.einsum(
        "te,de->td", grad_attended, out_mat, preferred_element_type=jnp.float32
    ).astype(jnp.bfloat16)
    grad_context = grad_context.reshape(row_count, block_len, HEADS, HEAD_DIM)
    grad_query, grad_window = lax.map(
        partial(attend_back, score_scale=score_scale),
        (query_b, window, same_segment, logsum, grad_context),
    )
    grad_kv = near_back(grad_window, block_len)
    grad_query_b = grad_query.reshape(tokens, features).astype(jnp.bfloat16)
    grad_kv_b = grad_kv.reshape(tokens, 2 * features).astype(jnp.bfloat16)
    grad_query_weight = jnp.einsum(
        "td,te->de", inputs, grad_query_b, preferred_element_type=jnp.float32
    )
    grad_query_bias = jnp.sum(grad_query_b.astype(jnp.float32), axis=0)
    grad_kv_weight = jnp.einsum("td,te->de", inputs, grad_kv_b, preferred_element_type=jnp.float32)
    grad_value_bias = jnp.sum(grad_kv_b[:, features:].astype(jnp.float32), axis=0)
    grad_in = grad_first + jnp.einsum(
        "te,de->td", grad_query_b, query_mat, preferred_element_type=jnp.float32
    )
    grad_in = grad_in + jnp.einsum(
        "te,de->td", grad_kv_b, kv_mat, preferred_element_type=jnp.float32
    )
    partial_grads = (
        grad_query_weight,
        grad_query_bias,
        grad_kv_weight[:, :features],
        grad_kv_weight[:, features:],
        grad_value_bias,
        grad_out_weight,
        grad_out_bias,
        grad_attn_gain,
        grad_attn_shift,
        grad_inner_weight,
        grad_inner_bias,
        grad_outer_weight,
        grad_outer_bias,
        grad_final_gain,
        grad_final_shift,
    )
    owned = (
        lax.psum_scatter(partial_grads[0], ("rows", "seq"), scatter_dimension=0, tiled=True),
        lax.psum_scatter(partial_grads[1], ("rows", "seq"), scatter_dimension=0, tiled=True),
        lax.psum_scatter(partial_grads[2], ("rows", "seq"), scatter_dimension=0, tiled=True),
        lax.psum_scatter(partial_grads[3], ("rows", "seq"), scatter_dimension=0, tiled=True),
        lax.psum_scatter(partial_grads[4], ("rows", "seq"), scatter_dimension=0, tiled=True),
        lax.psum_scatter(partial_grads[5], ("rows", "seq"), scatter_dimension=0, tiled=True),
        lax.psum_scatter(partial_grads[6], ("rows", "seq"), scatter_dimension=0, tiled=True),
        lax.psum_scatter(partial_grads[7], ("rows", "seq"), scatter_dimension=0, tiled=True),
        lax.psum_scatter(partial_grads[8], ("rows", "seq"), scatter_dimension=0, tiled=True),
        lax.psum_scatter(partial_grads[9], ("rows", "seq"), scatter_dimension=0, tiled=True),
        lax.psum_scatter(partial_grads[10], ("rows", "seq"), scatter_dimension=0, tiled=True),
        lax.psum_scatter(partial_grads[11], ("rows", "seq"), scatter_dimension=0, tiled=True),
        lax.psum_scatter(partial_grads[12], ("rows", "seq"), scatter_dimension=0, tiled=True),
        lax.psum_scatter(partial_grads[13], ("rows", "seq"), scatter_dimension=0, tiled=True),
        lax.psum_scatter(partial_grads[14], ("rows", "seq"), scatter_dimension=0, tiled=True),
    )
    g_qw, g_qb, g_kw, g_vw, g_vb, g_ow, g_ob, g_ag, g_as, g_iw, g_ib, g_tw, g_tb, g_fg, g_fs = owned
    return (
        layer_out.reshape(row_count, block_len, features),
        grad_in.reshape(row_count, block_len, features),
        g_qw,
        g_qb,
        g_kw,
        g_vw,
        g_vb,
        g_ow,
        g_ob,
        g_ag,
        g_as,
        g_iw,
        g_ib,
        g_tw,
        g_tb,
        g_fg,
        g_fs,
    )


def solution(mesh):
    placed = (
        P("rows", "seq", None),
        P("rows", "seq", None),
        P("rows", None),
        P(("rows", "seq"), None),
        P(("rows", "seq")),
        P(("rows", "seq"), None),
        P(("rows", "seq"), None),
        P(("rows", "seq")),
        P(("rows", "seq"), None),
        P(("rows", "seq")),
        P(("rows", "seq")),
        P(("rows", "seq")),
        P(("rows", "seq"), None),
        P(("rows", "seq")),
        P(("rows", "seq"), None),
        P(("rows", "seq")),
        P(("rows", "seq")),
        P(("rows", "seq")),
    )
    return jax.shard_map(
        body,
        mesh=mesh,
        in_specs=placed,
        out_specs=(
            P("rows", "seq", None),
            P("rows", "seq", None),
            P(("rows", "seq"), None),
            P(("rows", "seq")),
            P(("rows", "seq"), None),
            P(("rows", "seq"), None),
            P(("rows", "seq")),
            P(("rows", "seq"), None),
            P(("rows", "seq")),
            P(("rows", "seq")),
            P(("rows", "seq")),
            P(("rows", "seq"), None),
            P(("rows", "seq")),
            P(("rows", "seq"), None),
            P(("rows", "seq")),
            P(("rows", "seq")),
            P(("rows", "seq")),
        ),
        check_vma=False,
    )
```

profile of v0, /device:TPU:0, one launch (start us, length us, event | category | flops | bytes accessed | tf_op | source)
XLA Modules:
  0.0 1829.5 jit_solution(7902769398490669864)
XLA Ops:
  18.2 42.3 %all-reduce.20 = (bf16[768]{0:T(1024)(128)(2,1)S(1)}, bf16[768]{0:T(1024)(128)(2,1)S(1)}, bf16[768]{0:T(1024)(128)(2,1)S(1)}, bf16[768]{0:T(1024)(128)(2,1)S(1)}...) all-reduce(bf16[768]{0:T(1024)(128)(2,1)S(1)} %dynamic-update-slice, ...), channel_id=1, replica_groups=mesh['rows'=4,'seq'=8] {'rows','seq'}, use_global_device_ids=true, to_apply=%add.3 | all-reduce | flops 9216 | bytes 36864
  69.2 54.8 %all-gather.9.cloned.1.call-done = bf16[768,768]{1,0:T(8,128)(2,1)} async-done(((bf16[24,768]{1,0:T(8,128)(2,1)}), bf16[768,768]{1,0:T(8,128)(2,1)}) %all-gather.9.cloned.1.call-update) | async-done | bytes 1179664 | tf_op jit(solution)/shard_map/all_gather | solution.py:175
  155.5 104.2 %collective-permute-done = bf16[8,128,1536]{1,2,0:T(8,128)(2,1)S(1)} collective-permute-done((bf16[8,128,1536]{1,2,0:T(8,128)(2,1)}, bf16[8,128,1536]{1,2,0:T(8,128)(2,1)S(1)}, u32[]{:S(2)}, u32[]{:S(2)}) %collective-permute-start) | collective-permute-done | bytes 3145760 | tf_op jit(solution)/shard_map/ppermute | solution.py:17
  263.5 147.9 %all-gather.11.cloned.1.call-done = bf16[768,768]{1,0:T(8,128)(2,1)} async-done(((bf16[24,768]{1,0:T(8,128)(2,1)}), bf16[768,768]{1,0:T(8,128)(2,1)}) %all-gather.11.cloned.1.call-update) | async-done | bytes 1179664 | tf_op jit(solution)/shard_map/all_gather | solution.py:172
  443.2 64.7 %while.24 = (s32[]{:T(128)}, bf16[8,128,12,64]{1,3,2,0:T(8,128)(2,1)}, f32[8,12,128]{2,1,0:T(8,128)}, bf16[8,896,1536]{1,2,0:T(8,128)(2,1)}, pred[8,128,896]{2,1...) while((s32[]{:T(128)}, bf16[8,128,12,64]{1,3,2,0:T(8,128)(2,1)}, ...), condition=%wide.region_6.7_spmd, body=%wide.region_3.6_spmd.sunk | while | flops 368933376 | bytes 31295592 | solution.py:230
  518.9 60.8 %all-gather.15.cloned.1.call-done = bf16[768,3072]{1,0:T(8,128)(2,1)} async-done(((bf16[24,3072]{1,0:T(8,128)(2,1)}), bf16[768,3072]{1,0:T(8,128)(2,1)}) %all-gather.15.cloned.1.call-update) | async-done | bytes 4718608 | tf_op jit(solution)/shard_map/all_gather | solution.py:181
  579.7 35.8 %multiply_convert_fusion.1 = (bf16[1024,3072]{1,0:T(8,128)(2,1)}, f32[1024,3072]{1,0:T(8,128)}, f32[1024,3072]{1,0:T(8,128)}) fusion(f32[3072]{0:T(1024)S(1)} %convert_element_type.160, bf16[768,3072]{1,0:T(8,128)(2,1)} %all-gather.15.cloned.1.call-done, f32[1024,768]{1,0:T(8,128)S(1)} %get-tuple-element.300, f32[768]{0:T(1024)S(1)} %convert_element_type.158, ...), kind=kOutput, calls=%fused_computation.56 | convolution fusion | flops 5043388416 | bytes 39348224 | tf_op jit(solution)/shard_map/dot_general | solution.py:241
  615.5 28.9 %all-gather.17.cloned.1.call-done = bf16[3072,768]{1,0:T(8,128)(2,1)} async-done(((bf16[96,768]{1,0:T(8,128)(2,1)}), bf16[3072,768]{1,0:T(8,128)(2,1)}) %all-gather.17.cloned.1.call-update) | async-done | bytes 4718608 | tf_op jit(solution)/shard_map/all_gather | solution.py:183
  660.4 19.5 %convert_reduce_fusion = (f32[3072]{0:T(1024)}, bf16[1024,3072]{1,0:T(8,128)(2,1)}) fusion(f32[1024,3072]{1,0:T(8,128)} %get-tuple-element.280, bf16[3072,768]{1,0:T(8,128)(2,1)} %all-gather.17.cloned.1.call-done, f32[1024,768]{1,0:T(8,128)} %get-tuple-element.276, f32[1024,3072]{1,0:T(8,128)} %get-tuple-element.301, f32[3072]{0:T(1024)S(1)} %convert_element_type.160), kind=kOutput, calls=%fused_computation.54 | convolution fusion | flops 4886098944 | bytes 39346176 | tf_op jit(solution)/shard_map/td,fd->tf/dot_general | solution.py:263
  679.9 10.6 multiply_reduce_fusion.1
  697.6 225.8 %while.25 = (s32[]{:T(128)}, bf16[8,128,12,64]{1,3,2,0:T(8,128)(2,1)S(1)}, f32[8,896,1536]{2,1,0:T(8,128)}, bf16[8,896,1536]{1,2,0:T(8,128)(2,1)}, pred[8,128,89...) while((s32[]{:T(128)}, ...), condition=%wide.region_18.19_spmd, body=%wide.region_16.18_spmd.sunk | while | flops 903608832 | bytes 96761984 | solution.py:284
  923.4 23.9 %convert.8 = bf16[8,896,1536]{2,1,0:T(8,128)(2,1)} convert(f32[8,896,1536]{2,1,0:T(8,128)} %get-tuple-element.96) | non-fusion elementwise | flops 11010048 | bytes 66060288 | tf_op jit(solution)/shard_map/convert.5
  947.3 13.6 fusion.72
  984.4 52.0 %collective-permute-done.6 = bf16[8,128,1536]{2,1,0:T(8,128)(2,1)} collective-permute-done((bf16[8,128,1536]{2,1,0:T(8,128)(2,1)}, bf16[8,128,1536]{2,1,0:T(8,128)(2,1)}, u32[]{:S(2)}, u32[]{:S(2)}) %collective-permute-start.6) | collective-permute-done | bytes 3145760 | tf_op jit(solution)/shard_map/ppermute | solution.py:17
  1045.1 57.5 %collective-permute-done.11 = bf16[8,128,1536]{2,1,0:T(8,128)(2,1)} collective-permute-done((bf16[8,128,1536]{2,1,0:T(8,128)(2,1)}, bf16[8,128,1536]{2,1,0:T(8,128)(2,1)}, u32[]{:S(2)}, u32[]{:S(2)}) %collective-permute-start.11) | collective-permute-done | bytes 3145760 | tf_op jit(solution)/shard_map/ppermute | solution.py:17
  1102.6 68.6 %collective-permute-done.10 = bf16[8,128,1536]{2,1,0:T(8,128)(2,1)} collective-permute-done((bf16[8,128,1536]{2,1,0:T(8,128)(2,1)}, bf16[8,128,1536]{2,1,0:T(8,128)(2,1)}, u32[]{:S(2)}, u32[]{:S(2)}) %collective-permute-start.10) | collective-permute-done | bytes 3145760 | tf_op jit(solution)/shard_map/ppermute | solution.py:17
  1171.1 11.7 collective-permute-done.9
  1207.4 10.7 fusion.65
  1220.0 10.2 fusion.62
  1237.4 107.5 %all-reduce.19 = (f32[768]{0:T(1024)S(1)}, f32[768]{0:T(1024)S(1)}, f32[768]{0:T(1024)S(1)}, f32[768]{0:T(1024)S(1)}, f32[768]{0:T(1024)S(1)}, /*index=5*/f32[30...) all-reduce(f32[768]{0:T(1024)S(1)} %reduce_sum.212, ...), channel_id=3, replica_groups=mesh['rows'=4,'seq'=8] {'rows','seq'}, use_global_device_ids=true, to_apply=%region_21.22.clone | all-reduce | flops 9216 | bytes 73728
  1356.9 78.0 %reduce-scatter.23.cloned.1.call-done = f32[24,768]{1,0:T(8,128)} async-done(((f32[768,768]{1,0:T(8,128)}), f32[24,768]{1,0:T(8,128)}) %reduce-scatter.23.cloned.1.call-update) | async-done | bytes 73744
  1434.9 104.3 %reduce-scatter.21.cloned.1.call-done = f32[24,768]{1,0:T(8,128)} async-done(((f32[768,768]{1,0:T(8,128)}), f32[24,768]{1,0:T(8,128)}) %reduce-scatter.21.cloned.1.call-update) | async-done | bytes 73744
  1539.2 141.7 %reduce-scatter.15.cloned.1.call-done = f32[24,3072]{1,0:T(8,128)} async-done(((f32[768,3072]{1,0:T(8,128)}), f32[24,3072]{1,0:T(8,128)}) %reduce-scatter.15.cloned.1.call-update) | async-done | bytes 294928 | tf_op jit(solution)/shard_map/reduce_scatter | solution.py:330
  1680.9 141.5 %reduce-scatter.17.cloned.1.call-done = f32[96,768]{1,0:T(8,128)} async-done(((f32[3072,768]{1,0:T(8,128)}), f32[96,768]{1,0:T(8,128)}) %reduce-scatter.17.cloned.1.call-update) | async-done | bytes 294928 | tf_op jit(solution)/shard_map/reduce_scatter | solution.py:332
  (395 shorter events, 487.2 us)
Async XLA Ops:
  7.2 60.7 %all-gather.7.cloned.1.call-start = ((), (), s32[]{:S(2)}) async-start(), calls=%async_computation.6 | async-start | bytes 1216512 | tf_op jit(solution)/shard_map/all_gather | solution.py:174
  7.9 116.1 %all-gather.9.cloned.1.call-start = ((), (), s32[]{:S(2)}) async-start(), calls=%async_computation.7 | async-start | bytes 1216512 | tf_op jit(solution)/shard_map/all_gather | solution.py:175
  8.7 402.8 %all-gather.11.cloned.1.call-start = ((), (), s32[]{:S(2)}) async-start(), calls=%async_computation.8 | async-start | bytes 1216512 | tf_op jit(solution)/shard_map/all_gather | solution.py:172
  9.4 505.1 %all-gather.13.cloned.1.call-start = ((), (), s32[]{:S(2)}) async-start(), calls=%async_computation.9 | async-start | bytes 1216512 | tf_op jit(solution)/shard_map/all_gather | solution.py:177
  10.0 569.7 %all-gather.15.cloned.1.call-start = ((), (), s32[]{:S(2)}) async-start(), calls=%async_computation.10 | async-start | bytes 4866048 | tf_op jit(solution)/shard_map/all_gather | solution.py:181
  10.6 633.8 %all-gather.17.cloned.1.call-start = ((), (), s32[]{:S(2)}) async-start(), calls=%async_computation.11 | async-start | bytes 4866048 | tf_op jit(solution)/shard_map/all_gather | solution.py:183
  134.4 125.3 %collective-permute-start = (bf16[8,128,1536]{1,2,0:T(8,128)(2,1)}, bf16[8,128,1536]{1,2,0:T(8,128)(2,1)S(1)}, u32[]{:S(2)}, u32[]{:S(2)}) collective-permute-start(bf16[8,128,1536]{1,2,0:T(8,128)(2,1)} %copy.94), channel_id=1, source_target_pairs={{0,3},{1,4},{2,5},{3,6},{4,7},{8,11},{9,12},{10,13},{11,14},{12,15... | collective-permute-start | bytes 9437192 | tf_op jit(solution)/shard_map/ppermute | solution.py:17
  138.0 1218.9 %reduce-scatter.13.cloned.1.call-start = ((), (), s32[]{:S(2)}) async-start(), calls=%async_computation.12 | async-start | bytes 2433024 | tf_op jit(solution)/shard_map/reduce_scatter | solution.py:326
  138.1 281.8 %collective-permute-start.1 = (bf16[8,128,1536]{1,2,0:T(8,128)(2,1)}, bf16[8,128,1536]{1,2,0:T(8,128)(2,1)}, u32[]{:S(2)}, u32[]{:S(2)}) collective-permute-start(bf16[8,128,1536]{1,2,0:T(8,128)(2,1)} %copy.94), channel_id=1, source_target_pairs={{0,2},{1,3},{2,4},{3,5},{4,6},{5,7},{8,10},{9,11},{10,12},{11,13},... | collective-permute-start | bytes 9437192 | tf_op jit(solution)/shard_map/ppermute | solution.py:17
  142.7 279.8 %collective-permute-start.2 = (bf16[8,128,1536]{1,2,0:T(8,128)(2,1)}, bf16[8,128,1536]{1,2,0:T(8,128)(2,1)}, u32[]{:S(2)}, u32[]{:S(2)}) collective-permute-start(bf16[8,128,1536]{1,2,0:T(8,128)(2,1)} %copy.94), channel_id=1, source_target_pairs={{0,1},{1,2},{2,3},{3,4},{4,5},{5,6},{6,7},{8,9},{9,10},{10,11},{11... | collective-permute-start | bytes 9437192 | tf_op jit(solution)/shard_map/ppermute | solution.py:17
  152.2 275.7 %collective-permute-start.3 = (bf16[8,128,1536]{1,2,0:T(8,128)(2,1)}, bf16[8,128,1536]{1,2,0:T(8,128)(2,1)}, u32[]{:S(2)}, u32[]{:S(2)}) collective-permute-start(bf16[8,128,1536]{1,2,0:T(8,128)(2,1)} %copy.94), channel_id=1, source_target_pairs={{1,0},{2,1},{3,2},{4,3},{5,4},{6,5},{7,6},{9,8},{10,9},{11,10},{12... | collective-permute-start | bytes 9437192 | tf_op jit(solution)/shard_map/ppermute | solution.py:17
  153.6 277.0 %collective-permute-start.4 = (bf16[8,128,1536]{1,2,0:T(8,128)(2,1)}, bf16[8,128,1536]{1,2,0:T(8,128)(2,1)}, u32[]{:S(2)}, u32[]{:S(2)}) collective-permute-start(bf16[8,128,1536]{1,2,0:T(8,128)(2,1)} %copy.94), channel_id=1, source_target_pairs={{2,0},{3,1},{4,2},{5,3},{6,4},{7,5},{10,8},{11,9},{12,10},{13,11},... | collective-permute-start | bytes 9437192 | tf_op jit(solution)/shard_map/ppermute | solution.py:17
  259.7 173.6 %collective-permute-start.5 = (bf16[8,128,1536]{1,2,0:T(8,128)(2,1)}, bf16[8,128,1536]{1,2,0:T(8,128)(2,1)}, u32[]{:S(2)}, u32[]{:S(2)}) collective-permute-start(bf16[8,128,1536]{1,2,0:T(8,128)(2,1)} %copy.94), channel_id=1, source_target_pairs={{3,0},{4,1},{5,2},{6,3},{7,4},{11,8},{12,9},{13,10},{14,11},{15,12... | collective-permute-start | bytes 9437192 | tf_op jit(solution)/shard_map/ppermute | solution.py:17
  960.9 75.5 %collective-permute-start.6 = (bf16[8,128,1536]{2,1,0:T(8,128)(2,1)}, bf16[8,128,1536]{2,1,0:T(8,128)(2,1)}, u32[]{:S(2)}, u32[]{:S(2)}) collective-permute-start(bf16[8,128,1536]{2,1,0:T(8,128)(2,1)} %get-tuple-element.289), channel_id=1, source_target_pairs={{3,0},{4,1},{5,2},{6,3},{7,4},{11,8},{12,9},{13,10},{14,11},{15,12... | collective-permute-start | bytes 9437192 | tf_op jit(solution)/shard_map/ppermute | solution.py:17
  965.0 391.9 %reduce-scatter.19.cloned.1.call-start = ((), (), s32[]{:S(2)}) async-start(), calls=%async_computation.15 | async-start | bytes 2433024
  965.0 137.6 %collective-permute-start.11 = (bf16[8,128,1536]{2,1,0:T(8,128)(2,1)}, bf16[8,128,1536]{2,1,0:T(8,128)(2,1)}, u32[]{:S(2)}, u32[]{:S(2)}) collective-permute-start(bf16[8,128,1536]{2,1,0:T(8,128)(2,1)} %get-tuple-element.290), channel_id=1, source_target_pairs={{0,3},{1,4},{2,5},{3,6},{4,7},{8,11},{9,12},{10,13},{11,14},{12,15... | collective-permute-start | bytes 9437192 | tf_op jit(solution)/shard_map/ppermute | solution.py:17
  972.1 199.0 %collective-permute-start.10 = (bf16[8,128,1536]{2,1,0:T(8,128)(2,1)}, bf16[8,128,1536]{2,1,0:T(8,128)(2,1)}, u32[]{:S(2)}, u32[]{:S(2)}) collective-permute-start(bf16[8,128,1536]{2,1,0:T(8,128)(2,1)} %get-tuple-element.291), channel_id=1, source_target_pairs={{0,2},{1,3},{2,4},{3,5},{4,6},{5,7},{8,10},{9,11},{10,12},{11,13},... | collective-permute-start | bytes 9437192 | tf_op jit(solution)/shard_map/ppermute | solution.py:17
  978.7 204.1 %collective-permute-start.9 = (bf16[8,128,1536]{2,1,0:T(8,128)(2,1)}, bf16[8,128,1536]{2,1,0:T(8,128)(2,1)}, u32[]{:S(2)}, u32[]{:S(2)}) collective-permute-start(bf16[8,128,1536]{2,1,0:T(8,128)(2,1)} %get-tuple-element.292), channel_id=1, source_target_pairs={{0,1},{1,2},{2,3},{3,4},{4,5},{5,6},{6,7},{8,9},{9,10},{10,11},{11... | collective-permute-start | bytes 9437192 | tf_op jit(solution)/shard_map/ppermute | solution.py:17
  983.1 199.7 %collective-permute-start.8 = (bf16[8,128,1536]{2,1,0:T(8,128)(2,1)}, bf16[8,128,1536]{2,1,0:T(8,128)(2,1)}, u32[]{:S(2)}, u32[]{:S(2)}) collective-permute-start(bf16[8,128,1536]{2,1,0:T(8,128)(2,1)} %get-tuple-element.293), channel_id=1, source_target_pairs={{1,0},{2,1},{3,2},{4,3},{5,4},{6,5},{7,6},{9,8},{10,9},{11,10},{12... | collective-permute-start | bytes 9437192 | tf_op jit(solution)/shard_map/ppermute | solution.py:17
  1036.4 151.2 %collective-permute-start.7 = (bf16[8,128,1536]{2,1,0:T(8,128)(2,1)}, bf16[8,128,1536]{2,1,0:T(8,128)(2,1)}, u32[]{:S(2)}, u32[]{:S(2)}) collective-permute-start(bf16[8,128,1536]{2,1,0:T(8,128)(2,1)} %get-tuple-element.294), channel_id=1, source_target_pairs={{2,0},{3,1},{4,2},{5,3},{6,4},{7,5},{10,8},{11,9},{12,10},{13,11},... | collective-permute-start | bytes 9437192 | tf_op jit(solution)/shard_map/ppermute | solution.py:17
  1045.0 389.8 %reduce-scatter.23.cloned.1.call-start = ((), (), s32[]{:S(2)}) async-start(), calls=%async_computation.17 | async-start | bytes 2433024
  1203.9 335.3 %reduce-scatter.21.cloned.1.call-start = ((), (), s32[]{:S(2)}) async-start(), calls=%async_computation.16 | async-start | bytes 2433024
  1207.3 473.6 %reduce-scatter.15.cloned.1.call-start = ((), (), s32[]{:S(2)}) async-start(), calls=%async_computation.13 | async-start | bytes 9732096 | tf_op jit(solution)/shard_map/reduce_scatter | solution.py:330
  1218.1 604.3 %reduce-scatter.17.cloned.1.call-start = ((), (), s32[]{:S(2)}) async-start(), calls=%async_computation.14 | async-start | bytes 9732096 | tf_op jit(solution)/shard_map/reduce_scatter | solution.py:332
  (42 other events, 1975.3 us)
Sparse Core Ops, SparseCore 0:
  10.9 56.9 all-gather.6
  70.8 53.1 all-gather.8
  127.0 284.4 all-gather.10
  414.2 100.2 all-gather.12
  517.3 62.3 all-gather.14
  582.5 61.8 all-gather.16
  965.1 260.7 reduce-scatter.12
  1231.7 98.5 reduce-scatter.18
  1336.2 98.6 reduce-scatter.22
  1440.6 98.5 reduce-scatter.20
  1545.7 135.2 reduce-scatter.14
  1687.2 135.1 reduce-scatter.16
where the time goes:
time: 1840 us; the launch traced here: 1830 us
  waiting for transfers between devices  1070 us (58%)
  matrix products  228 us (12%)
  local copies, waits for them, and re-layouts  226 us (12%)
  blocking collectives  150 us (8%)
  other arithmetic  100 us (5%)
  starting transfers between devices  40.3 us (2%)
    ppermute x12, waiting for transfers between devices, passed_along(): return lax.ppermute(block, axis, route)  299 us
    unnamed x15, waiting for transfers between devices  186 us
    unnamed x2, blocking collectives  150 us
    all_gather x1, waiting for transfers between devices, body(): lax.all_gather(shards[0], ('rows', 'seq'), axis=0, tiled=True)  148 us
    reduce_scatter x1, waiting for transfers between devices, body(): lax.psum_scatter(partial_grads[9], ('rows', 'seq'), scatter_dimension=0,...  142 us
    reduce_scatter x1, waiting for transfers between devices, body(): lax.psum_scatter(partial_grads[11], ('rows', 'seq'), scatter_dimension=0,...  141 us
    dynamic_update_slice x16, local copies, waits for them, and re-layouts, body(): lax.map(partial(attend_back, score_scale=score_scale), (query_b, window,...  92 us
    all_gather x1, waiting for transfers between devices, body(): lax.all_gather(shards[9], ('rows', 'seq'), axis=0, tiled=True)  60.8 us
  transfers between devices with their start and end apart: 24, of which 16 were waited for; matrix products, arithmetic and copies ran while one was open for 12% of the time, Pallas kernels for 0%

commit v1 on v0

--- a/solution.py
+++ b/solution.py
@@ -9,6 +9,25 @@
 REACH = 3
 epsilon = 1e-12
 masked_score = -1e30
+
+
+def detail_indices(piece_in):
+    left_arr = lax.axis_size(("rows", "seq"))
+    current_block = lax.axis_index(("rows", "seq"))
+    upper, passed = (left_arr, current_block)
+    all_rows, n_now = (piece_in, 1)
+    while n_now < upper:
+        so_far_all = []
+        no = 0
+        while no < upper:
+            so_far_all.append((no, no ^ n_now))
+            no = no + 1
+        low = lax.ppermute(all_rows, ("rows", "seq"), so_far_all)
+        main = jnp.concatenate([all_rows, low], 0)
+        u_next = jnp.concatenate([low, all_rows], 0)
+        all_rows = jnp.where(passed & n_now == 0, main, u_next)
+        n_now = 2 * n_now
+    return all_rows
 
 
 def passed_along(block, axis, distance):
@@ -169,7 +188,7 @@
         final_shift,
     )
     gathered = (
-        lax.all_gather(shards[0], ("rows", "seq"), axis=0, tiled=True),
+        detail_indices(shards[0]),
         lax.all_gather(shards[1], ("rows", "seq"), axis=0, tiled=True),
         lax.all_gather(shards[2], ("rows", "seq"), axis=0, tiled=True),
         lax.all_gather(shards[3], ("rows", "seq"), axis=0, tiled=True),

time: 1840 us -> 1900 us (1.033)
  starting transfers between devices: 40.3 us -> 253 us
  waiting for transfers between devices: 1070 us -> 927 us
    all_gather x1 -> x0, waiting for transfers between devices: 148 us -> none  [body(): lax.all_gather(shards[0], ('rows', 'seq'), axis=0, tiled=True)]
    ppermute x12, starting transfers between devices: 39.7 us -> 181 us  [passed_along(): return lax.ppermute(block, axis, route)]
    ppermute x0 -> x5, starting transfers between devices: none -> 71.8 us  [detail_indices(): low = lax.ppermute(all_rows, ('rows', 'seq'), so_far_all)]
    all_gather x1, waiting for transfers between devices: 60.8 us -> 0.02 us  [body(): lax.all_gather(shards[9], ('rows', 'seq'), axis=0, tiled=True)]
    ppermute x12, waiting for transfers between devices: 299 us -> 331 us  [passed_along(): return lax.ppermute(block, axis, route)]
    all_gather x1, waiting for transfers between devices: 28.9 us -> 48 us  [body(): lax.all_gather(shards[11], ('rows', 'seq'), axis=0, tiled=True)]
    unnamed x15 -> x14, waiting for transfers between devices: 186 us -> 184 us
    unnamed x123 -> x129, local copies, waits for them, and re-layouts: 53.7 us -> 53.7 us
  transfers between devices with their start and end apart: 24 -> 28, of which waited for: 16 -> 18; matrix products, arithmetic and copies ran while one was open for 12% -> 12% of each run, Pallas kernels for 0% -> 0%
where the time goes in v1:
time: 1900 us; the launch traced here: 1890 us
  waiting for transfers between devices  927 us (49%)
  starting transfers between devices  253 us (13%)
  matrix products  228 us (12%)
  local copies, waits for them, and re-layouts  224 us (12%)
  blocking collectives  136 us (7%)
  other arithmetic  100 us (5%)
    ppermute x12, waiting for transfers between devices, passed_along(): return lax.ppermute(block, axis, route)  331 us
    unnamed x14, waiting for transfers between devices  184 us
    ppermute x12, starting transfers between devices, passed_along(): return lax.ppermute(block, axis, route)  181 us
    reduce_scatter x1, waiting for transfers between devices, body(): lax.psum_scatter(partial_grads[11], ('rows', 'seq'), scatter_dimension=0,...  142 us
    reduce_scatter x1, waiting for transfers between devices, body(): lax.psum_scatter(partial_grads[9], ('rows', 'seq'), scatter_dimension=0,...  142 us
    unnamed x2, blocking collectives  136 us
    dynamic_update_slice x16, local copies, waits for them, and re-layouts, body(): lax.map(partial(attend_back, score_scale=score_scale), (query_b, window,...  92.4 us
    ppermute x5, starting transfers between devices, detail_indices(): low = lax.ppermute(all_rows, ('rows', 'seq'), so_far_all)  71.8 us
  transfers between devices with their start and end apart: 28, of which 18 were waited for; matrix products, arithmetic and copies ran while one was open for 12% of the time, Pallas kernels for 0%

profile of v1, /device:TPU:0, one launch (start us, length us, event | category | flops | bytes accessed | tf_op | source)
XLA Modules:
  0.0 1886.1 jit_solution(2946182522844458332)
XLA Ops:
  17.6 42.6 %all-reduce.20 = (bf16[768]{0:T(1024)(128)(2,1)S(1)}, bf16[768]{0:T(1024)(128)(2,1)S(1)}, bf16[768]{0:T(1024)(128)(2,1)S(1)}, bf16[768]{0:T(1024)(128)(2,1)S(1)}...) all-reduce(bf16[768]{0:T(1024)(128)(2,1)S(1)} %dynamic-update-slice, ...), channel_id=1, replica_groups=mesh['rows'=4,'seq'=8] {'rows','seq'}, use_global_device_ids=true, to_apply=%add.3 | all-reduce | flops 9216 | bytes 36864
  69.3 54.6 %all-gather.8.cloned.1.call-done = bf16[768,768]{1,0:T(8,128)(2,1)} async-done(((bf16[24,768]{1,0:T(8,128)(2,1)}), bf16[768,768]{1,0:T(8,128)(2,1)}) %all-gather.8.cloned.1.call-update) | async-done | bytes 1179664 | tf_op jit(solution)/shard_map/all_gather | solution.py:194
  141.9 65.6 %collective-permute-start.7 = (bf16[48,768]{1,0:T(8,128)(2,1)S(1)}, bf16[48,768]{1,0:T(8,128)(2,1)S(1)}, u32[]{:S(2)}, u32[]{:S(2)}) collective-permute-start(bf16[48,768]{1,0:T(8,128)(2,1)S(1)} %maximum_select_fusion.6), channel_id=1, source_target_pairs={{0,2},{1,3},{2,0},{3,1},{4,6},{5,7},{6,4},{7,5},{8,10},{9,11},{10,... | collective-permute-start | bytes 221192 | tf_op jit(solution)/shard_map/ppermute | solution.py:25
  221.6 69.8 %collective-permute-start.2 = (bf16[8,128,1536]{1,2,0:T(8,128)(2,1)}, bf16[8,128,1536]{1,2,0:T(8,128)(2,1)}, u32[]{:S(2)}, u32[]{:S(2)}) collective-permute-start(bf16[8,128,1536]{1,2,0:T(8,128)(2,1)} %copy.92), channel_id=1, source_target_pairs={{0,1},{1,2},{2,3},{3,4},{4,5},{5,6},{6,7},{8,9},{9,10},{10,11},{11... | collective-permute-start | bytes 9437192 | tf_op jit(solution)/shard_map/ppermute | solution.py:36
  297.4 10.9 collective-permute-done.10
  322.7 116.4 %collective-permute-done.2 = bf16[8,128,1536]{1,2,0:T(8,128)(2,1)} collective-permute-done((bf16[8,128,1536]{1,2,0:T(8,128)(2,1)}, bf16[8,128,1536]{1,2,0:T(8,128)(2,1)}, u32[]{:S(2)}, u32[]{:S(2)}) %collective-permute-start.2) | collective-permute-done | bytes 3145760 | tf_op jit(solution)/shard_map/ppermute | solution.py:36
  457.8 11.1 collective-permute-done.5
  478.8 64.9 %while.24 = (s32[]{:T(128)}, bf16[8,128,12,64]{1,3,2,0:T(8,128)(2,1)}, f32[8,12,128]{2,1,0:T(8,128)}, bf16[8,896,1536]{1,2,0:T(8,128)(2,1)}, pred[8,128,896]{2,1...) while((s32[]{:T(128)}, bf16[8,128,12,64]{1,3,2,0:T(8,128)(2,1)}, ...), condition=%wide.region_6.7_spmd, body=%wide.region_3.6_spmd.sunk | while | flops 368933376 | bytes 31295592 | solution.py:249
  552.9 36.4 %multiply_convert_fusion.1 = (bf16[1024,3072]{1,0:T(8,128)(2,1)}, f32[1024,3072]{1,0:T(8,128)}, f32[1024,3072]{1,0:T(8,128)}) fusion(f32[3072]{0:T(1024)S(1)} %convert_element_type.164, bf16[768,3072]{1,0:T(8,128)(2,1)} %all-gather.12.cloned.1.call-done, f32[1024,768]{1,0:T(8,128)S(1)} %get-tuple-element.300, f32[768]{0:T(1024)S(1)} %convert_element_type.162, ...), kind=kOutput, calls=%fused_computation.56 | convolution fusion | flops 5043388416 | bytes 39348224 | tf_op jit(solution)/shard_map/dot_general | solution.py:260
  589.2 48.0 %all-gather.14.cloned.1.call-done = bf16[3072,768]{1,0:T(8,128)(2,1)} async-done(((bf16[96,768]{1,0:T(8,128)(2,1)}), bf16[3072,768]{1,0:T(8,128)(2,1)}) %all-gather.14.cloned.1.call-update) | async-done | bytes 4718608 | tf_op jit(solution)/shard_map/all_gather | solution.py:202
  653.4 19.2 %convert_reduce_fusion = (f32[3072]{0:T(1024)}, bf16[1024,3072]{1,0:T(8,128)(2,1)}) fusion(f32[1024,3072]{1,0:T(8,128)} %get-tuple-element.280, bf16[3072,768]{1,0:T(8,128)(2,1)} %all-gather.14.cloned.1.call-done, f32[1024,768]{1,0:T(8,128)} %get-tuple-element.276, f32[1024,3072]{1,0:T(8,128)} %get-tuple-element.301, f32[3072]{0:T(1024)S(1)} %convert_element_type.164), kind=kOutput, calls=%fused_computation.54 | convolution fusion | flops 4886098944 | bytes 39346176 | tf_op jit(solution)/shard_map/td,fd->tf/dot_general | solution.py:282
  690.4 225.9 %while.25 = (s32[]{:T(128)}, bf16[8,128,12,64]{1,3,2,0:T(8,128)(2,1)S(1)}, f32[8,896,1536]{2,1,0:T(8,128)}, bf16[8,896,1536]{1,2,0:T(8,128)(2,1)}, pred[8,128,89...) while((s32[]{:T(128)}, ...), condition=%wide.region_18.19_spmd, body=%wide.region_16.18_spmd.sunk | while | flops 903608832 | bytes 96761984 | solution.py:303
  916.3 23.9 %convert.8 = bf16[8,896,1536]{2,1,0:T(8,128)(2,1)} convert(f32[8,896,1536]{2,1,0:T(8,128)} %get-tuple-element.96) | non-fusion elementwise | flops 11010048 | bytes 66060288 | tf_op jit(solution)/shard_map/convert.5
  940.2 13.6 fusion.75
  957.9 15.9 collective-permute-start.16
  976.8 76.5 %collective-permute-start.14 = (bf16[8,128,1536]{2,1,0:T(8,128)(2,1)}, bf16[8,128,1536]{2,1,0:T(8,128)(2,1)}, u32[]{:S(2)}, u32[]{:S(2)}) collective-permute-start(bf16[8,128,1536]{2,1,0:T(8,128)(2,1)} %get-tuple-element.292), channel_id=1, source_target_pairs={{0,1},{1,2},{2,3},{3,4},{4,5},{5,6},{6,7},{8,9},{9,10},{10,11},{11... | collective-permute-start | bytes 9437192 | tf_op jit(solution)/shard_map/ppermute | solution.py:36
  1063.5 44.3 %collective-permute-done.16 = bf16[8,128,1536]{2,1,0:T(8,128)(2,1)} collective-permute-done((bf16[8,128,1536]{2,1,0:T(8,128)(2,1)}, bf16[8,128,1536]{2,1,0:T(8,128)(2,1)}, u32[]{:S(2)}, u32[]{:S(2)}) %collective-permute-start.16) | collective-permute-done | bytes 3145760 | tf_op jit(solution)/shard_map/ppermute | solution.py:36
  1107.8 66.4 %collective-permute-done.15 = bf16[8,128,1536]{2,1,0:T(8,128)(2,1)} collective-permute-done((bf16[8,128,1536]{2,1,0:T(8,128)(2,1)}, bf16[8,128,1536]{2,1,0:T(8,128)(2,1)}, u32[]{:S(2)}, u32[]{:S(2)}) %collective-permute-start.15) | collective-permute-done | bytes 3145760 | tf_op jit(solution)/shard_map/ppermute | solution.py:36
  1174.2 79.7 %collective-permute-done.14 = bf16[8,128,1536]{2,1,0:T(8,128)(2,1)} collective-permute-done((bf16[8,128,1536]{2,1,0:T(8,128)(2,1)}, bf16[8,128,1536]{2,1,0:T(8,128)(2,1)}, u32[]{:S(2)}, u32[]{:S(2)}) %collective-permute-start.14) | collective-permute-done | bytes 3145760 | tf_op jit(solution)/shard_map/ppermute | solution.py:36
  1309.4 93.7 %all-reduce.19 = (f32[768]{0:T(1024)S(1)}, f32[768]{0:T(1024)S(1)}, f32[768]{0:T(1024)S(1)}, f32[768]{0:T(1024)S(1)}, f32[768]{0:T(1024)S(1)}, /*index=5*/f32[30...) all-reduce(f32[768]{0:T(1024)S(1)} %reduce_sum.212, ...), channel_id=3, replica_groups=mesh['rows'=4,'seq'=8] {'rows','seq'}, use_global_device_ids=true, to_apply=%region_21.22.clone | all-reduce | flops 9216 | bytes 73728
  1415.1 76.7 %reduce-scatter.23.cloned.1.call-done = f32[24,768]{1,0:T(8,128)} async-done(((f32[768,768]{1,0:T(8,128)}), f32[24,768]{1,0:T(8,128)}) %reduce-scatter.23.cloned.1.call-update) | async-done | bytes 73744
  1491.8 104.4 %reduce-scatter.21.cloned.1.call-done = f32[24,768]{1,0:T(8,128)} async-done(((f32[768,768]{1,0:T(8,128)}), f32[24,768]{1,0:T(8,128)}) %reduce-scatter.21.cloned.1.call-update) | async-done | bytes 73744
  1596.2 141.5 %reduce-scatter.15.cloned.1.call-done = f32[24,3072]{1,0:T(8,128)} async-done(((f32[768,3072]{1,0:T(8,128)}), f32[24,3072]{1,0:T(8,128)}) %reduce-scatter.15.cloned.1.call-update) | async-done | bytes 294928 | tf_op jit(solution)/shard_map/reduce_scatter | solution.py:349
  1737.7 141.6 %reduce-scatter.17.cloned.1.call-done = f32[96,768]{1,0:T(8,128)} async-done(((f32[3072,768]{1,0:T(8,128)}), f32[96,768]{1,0:T(8,128)}) %reduce-scatter.17.cloned.1.call-update) | async-done | bytes 294928 | tf_op jit(solution)/shard_map/reduce_scatter | solution.py:351
  (411 shorter events, 517.1 us)
Async XLA Ops:
  7.9 116.0 %all-gather.8.cloned.1.call-start = ((), (), s32[]{:S(2)}) async-start(), calls=%async_computation.7 | async-start | bytes 1216512 | tf_op jit(solution)/shard_map/all_gather | solution.py:194
  8.7 539.7 %all-gather.10.cloned.1.call-start = ((), (), s32[]{:S(2)}) async-start(), calls=%async_computation.8 | async-start | bytes 1216512 | tf_op jit(solution)/shard_map/all_gather | solution.py:196
  9.4 543.4 %all-gather.12.cloned.1.call-start = ((), (), s32[]{:S(2)}) async-start(), calls=%async_computation.9 | async-start | bytes 4866048 | tf_op jit(solution)/shard_map/all_gather | solution.py:200
  10.0 627.3 %all-gather.14.cloned.1.call-start = ((), (), s32[]{:S(2)}) async-start(), calls=%async_computation.10 | async-start | bytes 4866048 | tf_op jit(solution)/shard_map/all_gather | solution.py:202
  134.3 175.9 %collective-permute-start = (bf16[8,128,1536]{1,2,0:T(8,128)(2,1)}, bf16[8,128,1536]{1,2,0:T(8,128)(2,1)S(1)}, u32[]{:S(2)}, u32[]{:S(2)}) collective-permute-start(bf16[8,128,1536]{1,2,0:T(8,128)(2,1)} %copy.92), channel_id=1, source_target_pairs={{0,3},{1,4},{2,5},{3,6},{4,7},{8,11},{9,12},{10,13},{11,14},{12,15... | collective-permute-start | bytes 9437192 | tf_op jit(solution)/shard_map/ppermute | solution.py:36
  139.0 1276.0 %reduce-scatter.13.cloned.1.call-start = ((), (), s32[]{:S(2)}) async-start(), calls=%async_computation.11 | async-start | bytes 2433024 | tf_op jit(solution)/shard_map/reduce_scatter | solution.py:345
  141.9 68.0 %collective-permute-start.7 = (bf16[48,768]{1,0:T(8,128)(2,1)S(1)}, bf16[48,768]{1,0:T(8,128)(2,1)S(1)}, u32[]{:S(2)}, u32[]{:S(2)}) collective-permute-start(bf16[48,768]{1,0:T(8,128)(2,1)S(1)} %maximum_select_fusion.6), channel_id=1, source_target_pairs={{0,2},{1,3},{2,0},{3,1},{4,6},{5,7},{6,4},{7,5},{8,10},{9,11},{10,... | collective-permute-start | bytes 221192 | tf_op jit(solution)/shard_map/ppermute | solution.py:25
  215.0 105.1 %collective-permute-start.1 = (bf16[8,128,1536]{1,2,0:T(8,128)(2,1)}, bf16[8,128,1536]{1,2,0:T(8,128)(2,1)}, u32[]{:S(2)}, u32[]{:S(2)}) collective-permute-start(bf16[8,128,1536]{1,2,0:T(8,128)(2,1)} %copy.92), channel_id=1, source_target_pairs={{0,2},{1,3},{2,4},{3,5},{4,6},{5,7},{8,10},{9,11},{10,12},{11,13},... | collective-permute-start | bytes 9437192 | tf_op jit(solution)/shard_map/ppermute | solution.py:36
  221.4 70.0 %collective-permute-start.9 = (bf16[192,768]{1,0:T(8,128)(2,1)S(1)}, bf16[192,768]{1,0:T(8,128)(2,1)S(1)}, u32[]{:S(2)}, u32[]{:S(2)}) collective-permute-start(bf16[192,768]{1,0:T(8,128)(2,1)S(1)} %maximum_select_fusion.2), channel_id=1, source_target_pairs={{0,8},{1,9},{2,10},{3,11},{4,12},{5,13},{6,14},{7,15},{8,0},{9,1},... | collective-permute-start | bytes 884744 | tf_op jit(solution)/shard_map/ppermute | solution.py:25
  221.6 217.6 %collective-permute-start.2 = (bf16[8,128,1536]{1,2,0:T(8,128)(2,1)}, bf16[8,128,1536]{1,2,0:T(8,128)(2,1)}, u32[]{:S(2)}, u32[]{:S(2)}) collective-permute-start(bf16[8,128,1536]{1,2,0:T(8,128)(2,1)} %copy.92), channel_id=1, source_target_pairs={{0,1},{1,2},{2,3},{3,4},{4,5},{5,6},{6,7},{8,9},{9,10},{10,11},{11... | collective-permute-start | bytes 9437192 | tf_op jit(solution)/shard_map/ppermute | solution.py:36
  296.1 148.4 %collective-permute-start.3 = (bf16[8,128,1536]{1,2,0:T(8,128)(2,1)}, bf16[8,128,1536]{1,2,0:T(8,128)(2,1)}, u32[]{:S(2)}, u32[]{:S(2)}) collective-permute-start(bf16[8,128,1536]{1,2,0:T(8,128)(2,1)} %copy.92), channel_id=1, source_target_pairs={{1,0},{2,1},{3,2},{4,3},{5,4},{6,5},{7,6},{9,8},{10,9},{11,10},{12... | collective-permute-start | bytes 9437192 | tf_op jit(solution)/shard_map/ppermute | solution.py:36
  308.3 146.8 %collective-permute-start.4 = (bf16[8,128,1536]{1,2,0:T(8,128)(2,1)}, bf16[8,128,1536]{1,2,0:T(8,128)(2,1)}, u32[]{:S(2)}, u32[]{:S(2)}) collective-permute-start(bf16[8,128,1536]{1,2,0:T(8,128)(2,1)} %copy.92), channel_id=1, source_target_pairs={{2,0},{3,1},{4,2},{5,3},{6,4},{7,5},{10,8},{11,9},{12,10},{13,11},... | collective-permute-start | bytes 9437192 | tf_op jit(solution)/shard_map/ppermute | solution.py:36
  310.2 158.6 %collective-permute-start.5 = (bf16[8,128,1536]{1,2,0:T(8,128)(2,1)}, bf16[8,128,1536]{1,2,0:T(8,128)(2,1)}, u32[]{:S(2)}, u32[]{:S(2)}) collective-permute-start(bf16[8,128,1536]{1,2,0:T(8,128)(2,1)} %copy.92), channel_id=1, source_target_pairs={{3,0},{4,1},{5,2},{6,3},{7,4},{11,8},{12,9},{13,10},{14,11},{15,12... | collective-permute-start | bytes 9437192 | tf_op jit(solution)/shard_map/ppermute | solution.py:36
  953.8 101.2 %collective-permute-start.11 = (bf16[8,128,1536]{2,1,0:T(8,128)(2,1)}, bf16[8,128,1536]{2,1,0:T(8,128)(2,1)}, u32[]{:S(2)}, u32[]{:S(2)}) collective-permute-start(bf16[8,128,1536]{2,1,0:T(8,128)(2,1)} %get-tuple-element.289), channel_id=1, source_target_pairs={{3,0},{4,1},{5,2},{6,3},{7,4},{11,8},{12,9},{13,10},{14,11},{15,12... | collective-permute-start | bytes 9437192 | tf_op jit(solution)/shard_map/ppermute | solution.py:36
  957.9 457.2 %reduce-scatter.19.cloned.1.call-start = ((), (), s32[]{:S(2)}) async-start(), calls=%async_computation.14 | async-start | bytes 2433024
  957.9 149.9 %collective-permute-start.16 = (bf16[8,128,1536]{2,1,0:T(8,128)(2,1)}, bf16[8,128,1536]{2,1,0:T(8,128)(2,1)}, u32[]{:S(2)}, u32[]{:S(2)}) collective-permute-start(bf16[8,128,1536]{2,1,0:T(8,128)(2,1)} %get-tuple-element.290), channel_id=1, source_target_pairs={{0,3},{1,4},{2,5},{3,6},{4,7},{8,11},{9,12},{10,13},{11,14},{12,15... | collective-permute-start | bytes 9437192 | tf_op jit(solution)/shard_map/ppermute | solution.py:36
  973.8 200.4 %collective-permute-start.15 = (bf16[8,128,1536]{2,1,0:T(8,128)(2,1)}, bf16[8,128,1536]{2,1,0:T(8,128)(2,1)}, u32[]{:S(2)}, u32[]{:S(2)}) collective-permute-start(bf16[8,128,1536]{2,1,0:T(8,128)(2,1)} %get-tuple-element.291), channel_id=1, source_target_pairs={{0,2},{1,3},{2,4},{3,5},{4,6},{5,7},{8,10},{9,11},{10,12},{11,13},... | collective-permute-start | bytes 9437192 | tf_op jit(solution)/shard_map/ppermute | solution.py:36
  976.8 277.2 %collective-permute-start.14 = (bf16[8,128,1536]{2,1,0:T(8,128)(2,1)}, bf16[8,128,1536]{2,1,0:T(8,128)(2,1)}, u32[]{:S(2)}, u32[]{:S(2)}) collective-permute-start(bf16[8,128,1536]{2,1,0:T(8,128)(2,1)} %get-tuple-element.292), channel_id=1, source_target_pairs={{0,1},{1,2},{2,3},{3,4},{4,5},{5,6},{6,7},{8,9},{9,10},{10,11},{11... | collective-permute-start | bytes 9437192 | tf_op jit(solution)/shard_map/ppermute | solution.py:36
  1053.3 200.7 %collective-permute-start.13 = (bf16[8,128,1536]{2,1,0:T(8,128)(2,1)}, bf16[8,128,1536]{2,1,0:T(8,128)(2,1)}, u32[]{:S(2)}, u32[]{:S(2)}) collective-permute-start(bf16[8,128,1536]{2,1,0:T(8,128)(2,1)} %get-tuple-element.293), channel_id=1, source_target_pairs={{1,0},{2,1},{3,2},{4,3},{5,4},{6,5},{7,6},{9,8},{10,9},{11,10},{12... | collective-permute-start | bytes 9437192 | tf_op jit(solution)/shard_map/ppermute | solution.py:36
  1055.0 204.3 %collective-permute-start.12 = (bf16[8,128,1536]{2,1,0:T(8,128)(2,1)}, bf16[8,128,1536]{2,1,0:T(8,128)(2,1)}, u32[]{:S(2)}, u32[]{:S(2)}) collective-permute-start(bf16[8,128,1536]{2,1,0:T(8,128)(2,1)} %get-tuple-element.294), channel_id=1, source_target_pairs={{2,0},{3,1},{4,2},{5,3},{6,4},{7,5},{10,8},{11,9},{12,10},{13,11},... | collective-permute-start | bytes 9437192 | tf_op jit(solution)/shard_map/ppermute | solution.py:36
  1063.5 428.3 %reduce-scatter.23.cloned.1.call-start = ((), (), s32[]{:S(2)}) async-start(), calls=%async_computation.16 | async-start | bytes 2433024
  1275.5 320.7 %reduce-scatter.21.cloned.1.call-start = ((), (), s32[]{:S(2)}) async-start(), calls=%async_computation.15 | async-start | bytes 2433024
  1278.9 458.9 %reduce-scatter.15.cloned.1.call-start = ((), (), s32[]{:S(2)}) async-start(), calls=%async_computation.12 | async-start | bytes 9732096 | tf_op jit(solution)/shard_map/reduce_scatter | solution.py:349
  1289.7 589.7 %reduce-scatter.17.cloned.1.call-start = ((), (), s32[]{:S(2)}) async-start(), calls=%async_computation.13 | async-start | bytes 9732096 | tf_op jit(solution)/shard_map/reduce_scatter | solution.py:351
  (49 other events, 1941.8 us)
Sparse Core Ops, SparseCore 0:
  10.9 57.0 all-gather.5
  70.9 53.0 all-gather.7
  126.9 180.0 all-gather.9
  309.7 209.6 all-gather.11
  522.1 115.0 all-gather.13
  958.0 324.5 reduce-scatter.12
  1288.5 98.6 reduce-scatter.18
  1393.1 98.6 reduce-scatter.22
  1497.6 98.5 reduce-scatter.20
  1602.5 135.1 reduce-scatter.14
  1744.2 135.1 reduce-scatter.16
